TPU v7x, 32 devices: a whole 2x2x4 slice. The times are simulated.
32 devices in a mesh: fsdp: 8 (over z, x), rep: 4 (over y, core).
Axes of the slice: x: 2, y: 2, z: 4, core: 2. Of those that a mesh axis runs over, the one named last changes fastest.
Arguments:
- partials: bfloat16 [4, 56, 1024, 1024], P('rep', None, 'fsdp'), may hold values from -400 to 400
- sketch: bfloat16 [8, 4, 2, 1024, 256], P('fsdp', 'rep'), may hold values from -3 to 3
- owner_table: int32 [56, 1], replicated, may hold values from 0 to 7; in each aligned block of 14 rows (0 to 13, 14 to 27, ...) at most 2 rows name the same one
Outputs:
- update: bfloat16 [56, 1024, 1024], P('rep', 'fsdp')
- new_sketch: bfloat16 [8, 4, 2, 1024, 256], P('fsdp', 'rep')
Inputs may be any that keep to these rules, and one draw needn't show every extreme that they name: `owner_table`: in each aligned slice of 14 blocks no owner holds more than 2 blocks; some owner holds exactly 2 in some slice.
All inputs are finite; a program needn't handle non-finite values.
Results may differ from a plain program's by a relative error of at most 0.015.
Values may be sent and summed in bfloat16 or wider, within the bound.
A program may use at most 128 MiB of HBM per device.

v0:
```python
import math

import jax
import jax.numpy as jnp
from jax import lax
from jax.sharding import PartitionSpec as P

NS_ITERS = 5


DECAY = 0.9
DAMPING = 64.0
FIRST_AXES = (((0,), (0,)), ((), ()))
LAST_AXES = (((1,), (1,)), ((), ()))


def inverse_root(matrix, epsilon):
    identity = jnp.eye(matrix.shape[0], dtype=jnp.float32)
    trace_sum = jnp.trace(matrix) + epsilon
    current = matrix / trace_sum
    inverse = identity
    for repeat in range(NS_ITERS):
        middle = 1.5 * identity - 0.5 * jnp.dot(inverse, current, precision=lax.Precision.HIGHEST)
        current = jnp.dot(current, middle, precision=lax.Precision.HIGHEST)
        inverse = jnp.dot(middle, inverse, precision=lax.Precision.HIGHEST)
    return inverse / jnp.sqrt(trace_sum)


def precondition(gradient, current_sketch):
    identity = jnp.eye(current_sketch.shape[1], dtype=jnp.float32)
    projected = lax.dot_general(
        gradient, current_sketch, FIRST_AXES, preferred_element_type=jnp.float32
    ).astype(jnp.bfloat16)
    gram_matrix = lax.dot_general(
        current_sketch, current_sketch, FIRST_AXES, preferred_element_type=jnp.float32
    ).astype(jnp.bfloat16)
    powered = DECAY * jnp.dot(
        current_sketch, gram_matrix, preferred_element_type=jnp.float32
    ) + jnp.dot(gradient, projected, preferred_element_type=jnp.float32)
    inner_gram = lax.dot_general(powered, powered, FIRST_AXES, precision=lax.Precision.HIGHEST)
    basis_full = jnp.dot(powered, inverse_root(inner_gram, 1e-06), precision=lax.Precision.HIGHEST)
    basis_low = basis_full.astype(jnp.bfloat16)
    coefficients = lax.dot_general(
        gradient, basis_low, FIRST_AXES, preferred_element_type=jnp.float32
    ).astype(jnp.bfloat16)
    alignment = lax.dot_general(
        current_sketch, basis_low, FIRST_AXES, preferred_element_type=jnp.float32
    )
    energy = DECAY * lax.dot_general(
        alignment, alignment, FIRST_AXES, precision=lax.Precision.HIGHEST
    ) + lax.dot_general(coefficients, coefficients, FIRST_AXES, preferred_element_type=jnp.float32)
    root_inverse = inverse_root(energy + DAMPING * identity, 0.0)
    inner_part = jnp.dot(energy, root_inverse, precision=lax.Precision.HIGHEST)
    new_block = jnp.dot(basis_full, inner_part, precision=lax.Precision.HIGHEST).astype(
        jnp.bfloat16
    )
    mix_matrix = math.sqrt(DAMPING) * root_inverse - identity
    side_terms = lax.dot_general(
        coefficients.astype(jnp.float32), mix_matrix, LAST_AXES, precision=lax.Precision.HIGHEST
    ).astype(jnp.bfloat16)
    update_block = (
        gradient.astype(jnp.float32)
        + lax.dot_general(basis_low, side_terms, LAST_AXES, preferred_element_type=jnp.float32)
    ).astype(jnp.bfloat16)
    return (update_block, new_block)


def squared_sum(values):
    wide = values.astype(jnp.float32)
    return jnp.sum(wide * wide)


def process_slot(slot_index, arrived, clip_factor, held_sketches, filled):
    block_width = arrived.shape[-1]
    gradient = (clip_factor * arrived.reshape(block_width, block_width).astype(jnp.float32)).astype(
        jnp.bfloat16
    )
    current_sketch = held_sketches[slot_index]
    active = slot_index < filled
    update_block, new_block = precondition(gradient, current_sketch)
    new_block = jnp.where(active, new_block, current_sketch)
    return (update_block, new_block)


def local(partials, sketch, owner_table):
    block_total = partials.shape[1]
    row_count = partials.shape[2]
    block_width = partials.shape[3]
    fsdp_count = lax.axis_size("fsdp")
    per_slice = block_total // lax.axis_size("rep")
    slot_count = sketch.shape[2]
    reduced = lax.psum_scatter(
        partials[0].astype(jnp.float32).astype(jnp.bfloat16), "rep", scatter_dimension=0, tiled=True
    )
    my_owners = lax.dynamic_slice_in_dim(
        owner_table[:, 0], lax.axis_index("rep") * per_slice, per_slice
    )
    positions = jnp.arange(per_slice, dtype=jnp.int32)
    same_owner = (my_owners[:, None] == my_owners[None, :]) & (
        positions[:, None] < positions[None, :]
    )
    rank_in = jnp.sum(same_owner.astype(jnp.int32), axis=0)
    target = rank_in * fsdp_count + my_owners
    selector = (
        target[None, :] == jnp.arange(slot_count * fsdp_count, dtype=jnp.int32)[:, None]
    ).astype(jnp.bfloat16)
    flattened = reduced.reshape(per_slice, row_count * block_width)
    outgoing = jnp.dot(selector, flattened, preferred_element_type=jnp.float32).astype(jnp.bfloat16)
    outgoing = outgoing.reshape(slot_count, fsdp_count, row_count, block_width)
    sum_squares = lax.psum(squared_sum(reduced), ("fsdp", "rep"))
    clip_limit = 0.5 * math.sqrt(block_total * block_width * block_width)
    clip_factor = jnp.minimum(1.0, clip_limit / jnp.sqrt(sum_squares + 1e-06))
    filled = jnp.sum((my_owners == lax.axis_index("fsdp")).astype(jnp.int32))
    held_sketches = sketch[0, 0]
    fresh_list = []
    incoming = lax.all_to_all(outgoing, "fsdp", split_axis=1, concat_axis=1, tiled=True)
    update_list = []
    for slot_index in range(slot_count):
        update_block, new_block = process_slot(
            slot_index, incoming[slot_index], clip_factor, held_sketches, filled
        )
        update_list.append(update_block)
        fresh_list.append(new_block)
    stacked = jnp.stack(update_list).reshape(slot_count, fsdp_count, row_count, block_width)
    returned = lax.all_to_all(stacked, "fsdp", split_axis=1, concat_axis=1, tiled=True)
    returned = returned.reshape(slot_count * fsdp_count, row_count * block_width)
    my_updates = lax.dot_general(
        selector, returned, FIRST_AXES, preferred_element_type=jnp.float32
    ).astype(jnp.bfloat16)
    my_updates = my_updates.reshape(per_slice, row_count, block_width)
    return (my_updates, jnp.stack(fresh_list)[None, None])


def solution(mesh):
    placed = (P("rep", None, "fsdp", None), P("fsdp", "rep", None, None, None), P())
    return jax.shard_map(
        local,
        mesh=mesh,
        in_specs=placed,
        out_specs=(P("rep", "fsdp", None), P("fsdp", "rep", None, None, None)),
        check_vma=False,
    )
```

profile of v0, /device:TPU:0, one launch (start us, length us, event | category | flops | bytes accessed | tf_op | source)
XLA Modules:
  0.0 441.3 jit_solution(7717073570326933660)
XLA Ops:
  7.2 0.7 reduce-scatter.2.cloned.1.call-update
  7.9 0.8 fusion.55
  8.8 118.5 %reduce-scatter.2.cloned.1.call-done = bf16[14,128,1024]{2,1,0:T(8,128)(2,1)} async-done(((bf16[56,128,1024]{2,1,0:T(8,128)(2,1)}), bf16[14,128,1024]{2,1,0:T(8,128)(2,1)}) %reduce-scatter.2.cloned.1.call-update) | async-done | bytes 3670032 | tf_op jit(solution)/shard_map/reduce_scatter | solution.py:92
  127.3 2.5 pad.4
  129.8 2.3 copy.28
  132.1 1.2 convolution_convert_fusion.1
  133.3 4.3 copy.20
  137.6 5.5 %all-to-all-start = ((bf16[2,8,128,1024]{3,2,0,1:T(8,128)(2,1)}), bf16[2,8,128,1024]{3,2,0,1:T(8,128)(2,1)}, u32[]{:S(2)}, u32[]{:S(2)}) async-start(bf16[2,8,128,1024]{3,2,0,1:T(8,128)(2,1)} %copy.20), calls=%async_computation.1 | async-start | bytes 8388608 | tf_op jit(solution)/shard_map/all_to_all | solution.py:116
  143.1 4.5 %multiply_reduce_fusion = f32[]{:T(128)} fusion(bf16[14,128,1024]{2,1,0:T(8,128)(2,1)} %reduce-scatter.2.cloned.1.call-done), kind=kLoop, calls=%fused_computation.2 | loop fusion | flops 5505023 | bytes 3670020 | tf_op jit(solution)/shard_map/reduce_sum | solution.py:70
  147.7 109.1 %psum.7 = f32[]{:T(128)} all-reduce(f32[]{:T(128)} %multiply_reduce_fusion), channel_id=1, replica_groups=mesh['fsdp'=8,'rep'=4] {'fsdp','rep'}, use_global_device_ids=true, to_apply=%region_3.0 | all-reduce | flops 1 | bytes 8 | tf_op jit(solution)/shard_map/psum | solution.py:110
  257.5 4.9 %multiply_convert_fusion.1 = (bf16[1,8,128,1024]{3,2,0,1:T(8,128)(2,1)}, bf16[1,8,128,1024]{3,2,0,1:T(8,128)(2,1)S(1)}) fusion(bf16[2,8,128,1024]{3,2,0,1:T(8,128)(2,1)} %all-to-all-done, f32[]{:T(128)S(6)} %min_shard_map.3), kind=kLoop, calls=%fused_computation.8 | loop fusion | flops 6291456 | bytes 8388612 | tf_op jit(solution)/shard_map/convert_element_type | solution.py:75
  262.4 1.3 copy-done.5
  263.7 3.3 fusion.11
  267.0 2.1 fusion.1
  269.1 1.6 select_reduce_fusion.1
  271.7 0.4 fusion.45
  272.4 0.4 select_subtract_fusion.8
  273.6 0.4 select_subtract_fusion.7
  275.9 0.4 select_subtract_fusion.5
  276.3 0.4 convolution_divide_fusion.1
  276.7 1.8 fusion.92
  278.9 1.0 convolution_convert_fusion.6
  279.8 0.8 copy-done.8
  281.0 1.0 select_reduce_fusion
  282.7 1.0 select_subtract_fusion.4
  283.7 1.0 fusion.46
  285.0 0.4 select_subtract_fusion.3
  286.1 0.4 select_subtract_fusion.2
  287.3 0.4 select_subtract_fusion.1
  288.1 1.1 fusion.99
  289.2 5.5 %fusion.10 = f32[1024,256]{0,1:T(8,128)} fusion(bf16[1024,1024]{1,0:T(8,128)(2,1)} %bitcast.197, bf16[1,1,2,1024,256]{4,3,2,1,0:T(8,128)(2,1)S(1)} %copy-done), kind=kOutput, calls=%fused_computation.77 | convolution fusion | flops 1074003968 | bytes 5767168 | tf_op jit(solution)/shard_map/dot_general | solution.py:39
  294.7 2.1 fusion.3
  296.8 2.4 select_reduce_fusion.3
  299.9 1.3 select_subtract_fusion.19
  301.1 1.3 fusion.44
  302.8 0.4 select_subtract_fusion.18
  305.1 0.6 select_subtract_fusion.16
  306.9 0.4 convolution_divide_fusion.3
  307.3 1.8 fusion.78
  309.4 0.8 convolution_convert_fusion.8
  310.6 1.0 select_reduce_fusion.2
  312.2 0.9 select_subtract_fusion.14
  313.1 1.0 fusion.49
  314.4 0.4 select_subtract_fusion.13
  315.6 0.4 select_subtract_fusion.12
  316.8 0.4 select_subtract_fusion.11
  318.7 0.7 copy-done.13
  319.4 0.6 convolution_convert_fusion.4
  320.1 0.7 add_convert_fusion
  321.9 0.6 convolution_convert_fusion.5
  322.6 0.7 add_convert_fusion.1
  323.3 2.3 pad_maximum_fusion
  325.7 4.7 %all-to-all-start.1 = ((bf16[2,8,128,1024]{3,2,0,1:T(8,128)(2,1)}), bf16[2,8,128,1024]{3,2,0,1:T(8,128)(2,1)}, u32[]{:S(2)}, u32[]{:S(2)}) async-start(bf16[2,8,128,1024]{3,2,0,1:T(8,128)(2,1)} %pad_maximum_fusion), calls=%async_computation.2 | async-start | bytes 8388608 | tf_op jit(solution)/shard_map/all_to_all | solution.py:125
  331.8 1.3 fusion.101
  333.1 1.0 fusion.7
  334.1 1.4 fusion.100
  335.5 1.0 fusion.5
  336.5 1.1 maximum_bitcast_fusion
  337.6 85.4 %all-to-all-done.1 = bf16[2,8,128,1024]{3,2,0,1:T(8,128)(2,1)} async-done(((bf16[2,8,128,1024]{3,2,0,1:T(8,128)(2,1)}), bf16[2,8,128,1024]{3,2,0,1:T(8,128)(2,1)}, u32[]{:S(2)}, u32[]{:S(2)}) %all-to-all-start.1) | async-done | bytes 4194336 | tf_op jit(solution)/shard_map/all_to_all | solution.py:125
  423.0 2.6 copy.32
  425.6 2.3 copy.29
  428.0 1.5 convolution_convert_fusion
  429.5 2.3 copy.30
  431.8 2.2 slice.20
  (78 shorter events, 14.6 us)
Async XLA Ops:
  7.2 120.1 %reduce-scatter.2.cloned.1.call-start = ((), (), s32[]{:S(2)}) async-start(), calls=%async_computation.3 | async-start | bytes 18350080 | tf_op jit(solution)/shard_map/reduce_scatter | solution.py:92
  7.2 0.7 copy-start.18
  137.6 119.8 %all-to-all-start = ((bf16[2,8,128,1024]{3,2,0,1:T(8,128)(2,1)}), bf16[2,8,128,1024]{3,2,0,1:T(8,128)(2,1)}, u32[]{:S(2)}, u32[]{:S(2)}) async-start(bf16[2,8,128,1024]{3,2,0,1:T(8,128)(2,1)} %copy.20), calls=%async_computation.1 | async-start | bytes 8388608 | tf_op jit(solution)/shard_map/all_to_all | solution.py:116
  257.4 6.3 %copy-start = (bf16[1,1,2,1024,256]{4,3,2,1,0:T(8,128)(2,1)S(1)}, bf16[1,1,2,1024,256]{4,3,2,1,0:T(8,128)(2,1)}, u32[]{:S(2)}) copy-start(bf16[1,1,2,1024,256]{4,3,2,1,0:T(8,128)(2,1)} %param.4) | copy-start | bytes 3145732
  262.4 1.3 copy-start.5
  274.7 4.1 copy-start.6
  279.8 0.8 copy-start.8
  282.0 5.7 %copy-start.16 = (f32[256,256]{1,0:T(8,128)}, f32[256,256]{1,0:T(8,128)S(1)}, u32[]{:S(2)}) copy-start(f32[256,256]{1,0:T(8,128)S(1)} %get-tuple-element.9) | copy-start | bytes 786436
  305.1 4.3 copy-start.3
  309.1 1.5 copy-start.1
  310.2 1.4 copy-start.10
  311.6 5.5 %copy-start.17 = (f32[256,256]{1,0:T(8,128)}, f32[256,256]{1,0:T(8,128)S(1)}, u32[]{:S(2)}) copy-start(f32[256,256]{1,0:T(8,128)S(1)} %get-tuple-element.13) | copy-start | bytes 786436
  313.1 4.8 %copy-start.12 = (f32[256,256]{1,0:T(8,128)S(1)}, f32[256,256]{1,0:T(8,128)}, u32[]{:S(2)}) copy-start(f32[256,256]{1,0:T(8,128)} %fusion.99) | copy-start | bytes 786436
  314.8 4.6 %copy-start.9 = (bf16[1024,256]{1,0:T(8,128)(2,1)S(1)}, bf16[1024,256]{1,0:T(8,128)(2,1)}, u32[]{:S(2)}) copy-start(bf16[1024,256]{1,0:T(8,128)(2,1)} %copy-done.8) | copy-start | bytes 1572868
  315.2 4.9 %copy-start.7 = (bf16[1,8,128,1024]{3,2,0,1:T(8,128)(2,1)S(1)}, bf16[1,8,128,1024]{3,2,0,1:T(8,128)(2,1)}, u32[]{:S(2)}) copy-start(bf16[1,8,128,1024]{3,2,0,1:T(8,128)(2,1)} %copy-done.5) | copy-start | bytes 6291460
  318.7 0.7 copy-start.13
  319.4 2.2 copy-start.11
  320.1 2.5 copy-start.2
  320.1 2.5 copy-start.4
  321.7 1.7 copy-start.15
  325.7 6.1 %copy-start.14 = (f32[256,256]{1,0:T(8,128)S(1)}, f32[256,256]{1,0:T(8,128)}, u32[]{:S(2)}) copy-start(f32[256,256]{1,0:T(8,128)} %copy-done.13) | copy-start | bytes 786436
  325.7 97.3 %all-to-all-start.1 = ((bf16[2,8,128,1024]{3,2,0,1:T(8,128)(2,1)}), bf16[2,8,128,1024]{3,2,0,1:T(8,128)(2,1)}, u32[]{:S(2)}, u32[]{:S(2)}) async-start(bf16[2,8,128,1024]{3,2,0,1:T(8,128)(2,1)} %pad_maximum_fusion), calls=%async_computation.2 | async-start | bytes 8388608 | tf_op jit(solution)/shard_map/all_to_all | solution.py:125
Sparse Core Ops, SparseCore 0:
  10.6 116.6 reduce-scatter.1
where the time goes:
time: 448 us; the launch traced here: 441 us
  waiting for transfers between devices  205 us (46%)
  blocking collectives  109 us (24%)
  matrix products  61.9 us (14%)
  local copies, waits for them, and re-layouts  21.8 us (5%)
  between operations  20.1 us (4%)
  other arithmetic  13.8 us (3%)
  starting transfers between devices  10.2 us (2%)
    reduce_scatter x1, waiting for transfers between devices, local(): lax.psum_scatter(partials[0].astype(jnp.float32).astype(jnp.bfloat16), 'r...  118 us
    psum x1, blocking collectives, local(): sum_squares = lax.psum(squared_sum(reduced), ('fsdp', 'rep'))  109 us
    all_to_all x1, waiting for transfers between devices, local(): lax.all_to_all(stacked, 'fsdp', split_axis=1, concat_axis=1, tiled=True)  85.4 us
    unnamed x42, local copies, waits for them, and re-layouts  12.6 us
    dot_general x20, matrix products, inverse_root(): jnp.dot(inverse, current, precision=lax.Precision.HIGHEST)  9.76 us
    dot_general x16, matrix products, inverse_root(): current = jnp.dot(current, middle, precision=lax.Precision.HIGHEST)  9 us
  transfers between devices with their start and end apart: 3, of which 2 were waited for; matrix products, arithmetic and copies ran while one was open for 3% of the time, Pallas kernels for 0%

commit v1 on v0

--- a/solution.py
+++ b/solution.py
@@ -1,8 +1,11 @@
+import functools
 import math
 
 import jax
 import jax.numpy as jnp
 from jax import lax
+from jax.experimental import pallas as pl
+from jax.experimental.pallas import tpu as pltpu
 from jax.sharding import PartitionSpec as P
 
 NS_ITERS = 5
@@ -130,11 +133,467 @@
     my_updates = my_updates.reshape(per_slice, row_count, block_width)
     return (my_updates, jnp.stack(fresh_list)[None, None])
 
+MESH = pl.DeviceIdType.MESH
+BF = jnp.bfloat16
+F32 = jnp.float32
+
+
+def flip(value, mask, bits):
+    result = 0
+    for bit in range(bits):
+        ours = (value // (1 << bit)) % 2
+        theirs = (mask // (1 << bit)) % 2
+        result = result + (ours + theirs - 2 * ours * theirs) * (1 << bit)
+    return result
+
+
+def greet(peers):
+    barrier = pltpu.get_barrier_semaphore()
+    for peer in peers:
+        pl.semaphore_signal(barrier, inc=1, device_id=peer, device_id_type=MESH)
+    pl.semaphore_wait(barrier, len(peers))
+
+
+def remote(source, target, send_sem, recv_sem, peer):
+    return pltpu.make_async_remote_copy(
+        src_ref=source,
+        dst_ref=target,
+        send_sem=send_sem,
+        recv_sem=recv_sem,
+        device_id=peer,
+        device_id_type=MESH,
+    )
+
+
+def forward_kernel(
+    fsdp, slots, index_ref, valid_ref, partials_ref, incoming_ref, squares_ref,
+    held, staged, paired, far, crossed, summed, square_acc, rep_squares, fsdp_squares,
+    load_sem, pair_sems, cross_sems, owner_sems, self_sem, rep_sems, fsdp_sems,
+):
+    bits = fsdp.bit_length() - 1
+    half = fsdp // 2
+    steps = slots * fsdp
+    me_f = lax.axis_index("fsdp")
+    me_r = lax.axis_index("rep")
+    core = me_r % 2
+    row = me_r // 2
+    partner = row * 2 + 1 - core
+    across = (1 - row) * 2 + core
+    partner_across = (1 - row) * 2 + 1 - core
+
+    load = pltpu.make_async_copy(partials_ref.at[0], held, load_sem)
+    load.start()
+    greet(
+        [{"rep": (me_r + d) % 4} for d in range(1, 4)]
+        + [{"fsdp": (me_f + d) % fsdp} for d in range(1, fsdp)]
+    )
+    load.wait()
+
+    def where(i):
+        group = i // (slots * half)
+        slot = (i % (slots * half)) // half
+        mask = fsdp - 1 - half * group - i % half
+        return slot, mask, flip(me_f, mask, bits)
+
+    def pair_copy(i):
+        return remote(
+            staged.at[i], paired.at[i], pair_sems.at[0, i], pair_sems.at[1, i], {"rep": partner}
+        )
+
+    def cross_copy(i):
+        return remote(
+            far.at[i], crossed.at[i], cross_sems.at[0, i], cross_sems.at[1, i], {"rep": across}
+        )
+
+    def owner_copy(i):
+        slot, mask, owner = where(i)
+        return remote(
+            summed.at[i],
+            incoming_ref.at[slot, me_f],
+            owner_sems.at[0, i],
+            owner_sems.at[1, i],
+            {"fsdp": owner},
+        )
+
+    def self_copy(i):
+        slot, mask, owner = where(i)
+        return pltpu.make_async_copy(
+            summed.at[i], incoming_ref.at[slot, me_f], self_sem.at[slot]
+        )
+
+    def stage(i, carry):
+        slot, mask, owner = where(i)
+        place = slot * fsdp + owner
+        staged[i, 0] = held[index_ref[partner_across, place]]
+        staged[i, 1] = held[index_ref[partner, place]]
+        pair_copy(i).start()
+        return carry
+
+    lax.fori_loop(0, steps, stage, 0)
+    square_acc[...] = jnp.zeros_like(square_acc)
+
+    def send_across(i):
+        slot, mask, owner = where(i)
+        place = slot * fsdp + owner
+        pair_copy(i).wait_recv()
+        mine = held[index_ref[across, place]].astype(F32)
+        far[i] = (mine + paired[i, 0].astype(F32)).astype(BF)
+        cross_copy(i).start()
+
+    def send_owner(i):
+        slot, mask, owner = where(i)
+        place = slot * fsdp + owner
+        cross_copy(i).wait_recv()
+        mine = held[index_ref[me_r, place]].astype(F32)
+        total = (mine + paired[i, 1].astype(F32) + crossed[i].astype(F32)).astype(BF)
+        summed[i] = total
+
+        @pl.when(mask == 0)
+        def _():
+            self_copy(i).start()
+
+        @pl.when(mask != 0)
+        def _():
+            owner_copy(i).start()
+
+        wide = total.astype(F32)
+        folded = jnp.sum((wide * wide).reshape(wide.shape[0] // 8, 8, wide.shape[1]), axis=0)
+        square_acc[...] += folded * valid_ref[me_r, place]
+
+    lag = 2
+
+    def both(i, carry):
+        @pl.when(i < steps)
+        def _():
+            send_across(i)
+
+        @pl.when(i >= lag)
+        def _():
+            send_owner(i - lag)
+
+        return carry
+
+    lax.fori_loop(0, steps + lag, both, 0)
+
+    lanes = square_acc[:, 0:128]
+    for part in range(1, square_acc.shape[1] // 128):
+        lanes = lanes + square_acc[:, part * 128 : (part + 1) * 128]
+    rep_squares[me_r] = lanes
+    copies = [
+        remote(
+            rep_squares.at[me_r], rep_squares.at[me_r], rep_sems.at[0, d], rep_sems.at[1, d],
+            {"rep": (me_r + d) % 4},
+        )
+        for d in range(1, 4)
+    ]
+    for copy in copies:
+        copy.start()
+    for copy in copies:
+        copy.wait()
+    lanes = rep_squares[0]
+    for r in range(1, 4):
+        lanes = lanes + rep_squares[r]
+    fsdp_squares[me_f] = lanes
+    copies = [
+        remote(
+            fsdp_squares.at[me_f], fsdp_squares.at[me_f], fsdp_sems.at[0, d], fsdp_sems.at[1, d],
+            {"fsdp": (me_f + d) % fsdp},
+        )
+        for d in range(1, fsdp)
+    ]
+    for copy in copies:
+        copy.start()
+    for copy in copies:
+        copy.wait()
+    lanes = fsdp_squares[0]
+    for f in range(1, fsdp):
+        lanes = lanes + fsdp_squares[f]
+    squares_ref[...] = lanes
+
+    def finish(i, carry):
+        slot, mask, owner = where(i)
+        pair_copy(i).wait_send()
+        cross_copy(i).wait_send()
+
+        @pl.when(mask == 0)
+        def _():
+            self_copy(i).wait()
+
+        @pl.when(mask != 0)
+        def _():
+            owner_copy(i).wait()
+
+        return carry
+
+    lax.fori_loop(0, steps, finish, 0)
+
+
+def mm(a, b):
+    return jnp.dot(a, b, preferred_element_type=F32)
+
+
+def mm_last(a, b):
+    return lax.dot_general(a, b, LAST_AXES, preferred_element_type=F32)
+
+
+def split(values):
+    high = values.astype(BF)
+    return high, (values - high.astype(F32)).astype(BF)
+
+
+def mm3(a, b):
+    return mm(a[0], b[0]) + (mm(a[0], b[1]) + mm(a[1], b[0]))
+
+
+def eye_of(size):
+    return (
+        lax.broadcasted_iota(jnp.int32, (size, size), 0)
+        == lax.broadcasted_iota(jnp.int32, (size, size), 1)
+    ).astype(F32)
+
+
+def kernel_root(matrix, epsilon, identity):
+    trace_sum = jnp.sum(matrix * identity, keepdims=True) + epsilon
+    current = matrix / trace_sum
+    middle = 1.5 * identity - 0.5 * current
+    middle_s = split(middle)
+    inverse_s = middle_s
+    current_s = split(mm3(split(current), middle_s))
+    for repeat in range(1, NS_ITERS):
+        middle_s = split(1.5 * identity - 0.5 * mm3(inverse_s, current_s))
+        if repeat < NS_ITERS - 1:
+            current_s = split(mm3(current_s, middle_s))
+        inverse = mm3(middle_s, inverse_s)
+        inverse_s = split(inverse)
+    return inverse / jnp.sqrt(trace_sum)
+
+
+def owner_kernel(
+    fsdp, slots, clip_limit, active_ref, squares_ref, incoming_ref, sketch_ref, returned_ref, fresh_ref,
+    held, updates, narrow_t, side_t, wide, basis, basis_low, load_sem, send_sems, recv_sems, self_sem,
+):
+    bits = fsdp.bit_length() - 1
+    me_f = lax.axis_index("fsdp")
+    rows = held.shape[2]
+    width = held.shape[3]
+    rank = sketch_ref.shape[2]
+    tile = rank
+    loads = [
+        pltpu.make_async_copy(incoming_ref.at[k], held.at[k], load_sem.at[k]) for k in range(slots)
+    ]
+    for copy in loads:
+        copy.start()
+    greet([{"fsdp": (me_f + d) % fsdp} for d in range(1, fsdp)])
+    sum_squares = jnp.sum(squares_ref[...], keepdims=True)
+    clip_factor = jnp.minimum(1.0, clip_limit / jnp.sqrt(sum_squares + 1e-06))
+    identity = eye_of(rank)
+
+    def home_copy(k, i):
+        home = flip(me_f, fsdp - 1 - i, bits)
+        return remote(
+            updates.at[k, i], returned_ref.at[k, me_f], send_sems.at[k, i], recv_sems.at[k, i],
+            {"fsdp": home},
+        )
+
+    def self_copy(k):
+        return pltpu.make_async_copy(
+            updates.at[k, fsdp - 1], returned_ref.at[k, me_f], self_sem.at[k]
+        )
+
+    for k in range(slots):
+        loads[k].wait()
+        for part in range(fsdp):
+            held[k, part] = (clip_factor * held[k, part].astype(F32)).astype(BF)
+        sketch = sketch_ref[k]
+        sketch_t = sketch.T
+
+        def wide_part(part):
+            return held[k, :, :, part * tile : (part + 1) * tile].reshape(width, tile)
+
+        for part in range(width // tile):
+            narrow_t[:, part * tile : (part + 1) * tile] = mm(sketch_t, wide_part(part)).astype(BF)
+        gram = mm(sketch_t, sketch).astype(BF)
+        projected_t = narrow_t[...]
+        for part in range(fsdp):
+            span = slice(part * rows, (part + 1) * rows)
+            wide[span] = DECAY * mm(sketch[span], gram) + mm_last(held[k, part], projected_t)
+        powered_s = split(wide[...])
+        powered_t = powered_s[0].T
+        mixed = mm(powered_t, powered_s[1])
+        inner = mm(powered_t, powered_s[0]) + (mixed + mixed.T)
+        root = split(kernel_root(inner, 1e-06, identity))
+        full = mm3(powered_s, root)
+        basis[...] = full
+        low = full.astype(BF)
+        basis_low[...] = low
+        low_t = low.T
+        for part in range(width // tile):
+            narrow_t[:, part * tile : (part + 1) * tile] = mm(low_t, wide_part(part)).astype(BF)
+        coefficients_t = narrow_t[...]
+        alignment = mm(sketch_t, low)
+        align_s = split(alignment)
+        align_t = (align_s[0].T, align_s[1].T)
+        energy = DECAY * mm3(align_t, align_s) + mm_last(coefficients_t, coefficients_t)
+        root_inverse = kernel_root(energy + DAMPING * identity, 0.0, identity)
+        mix = split(math.sqrt(DAMPING) * root_inverse - identity)
+        side_t[...] = (mm(mix[0], coefficients_t) + mm(mix[1], coefficients_t)).astype(BF)
+
+        def send(i, carry):
+            home = flip(me_f, fsdp - 1 - i, bits)
+            start = pl.multiple_of(home * rows, rows)
+            updates[k, i] = (
+                held[k, home].astype(F32) + mm(basis_low[pl.ds(start, rows), :], side_t[...])
+            ).astype(BF)
+
+            @pl.when(i == fsdp - 1)
+            def _():
+                self_copy(k).start()
+
+            @pl.when(i != fsdp - 1)
+            def _():
+                home_copy(k, i).start()
+
+            return carry
+
+        lax.fori_loop(0, fsdp, send, 0)
+        inner_part = split(mm3(split(energy), split(root_inverse)))
+        new_block = mm3(split(basis[...]), inner_part).astype(BF)
+        fresh_ref[k] = jnp.where(active_ref[k] > 0, new_block, sketch)
+
+    def finish(i, carry):
+        for k in range(slots):
+            home_copy(k, i).wait()
+        return carry
+
+    lax.fori_loop(0, fsdp - 1, finish, 0)
+    for k in range(slots):
+        self_copy(k).wait()
+
+
+def place_kernel(target_ref, returned_ref, update_ref):
+    update_ref[...] = returned_ref[...]
+
+
+def fused(partials, sketch, owner_table):
+    block_total, rows, width = partials.shape[1:]
+    rank = sketch.shape[4]
+    fsdp = lax.axis_size("fsdp")
+    rep = lax.axis_size("rep")
+    slots = sketch.shape[2]
+    per_slice = block_total // rep
+    steps = slots * fsdp
+    owners = owner_table[:, 0].reshape(rep, per_slice)
+    positions = jnp.arange(per_slice, dtype=jnp.int32)
+    same = (owners[:, :, None] == owners[:, None, :]) & (positions[:, None] < positions[None, :])
+    target = jnp.sum(same.astype(jnp.int32), axis=1) * fsdp + owners
+    hit = target[:, None, :] == jnp.arange(steps, dtype=jnp.int32)[:, None]
+    numbers = jnp.arange(block_total, dtype=jnp.int32).reshape(rep, 1, per_slice)
+    index = jnp.sum(jnp.where(hit, numbers, 0), axis=2)
+    valid = jnp.sum(hit.astype(F32), axis=2)
+    me_r = lax.axis_index("rep")
+    my_target = lax.dynamic_index_in_dim(target, me_r, 0, keepdims=False)
+    active = lax.dynamic_slice(
+        lax.dynamic_index_in_dim(valid, me_r, 0, keepdims=False).reshape(slots, fsdp),
+        (0, lax.axis_index("fsdp")), (slots, 1),
+    )[:, 0]
+
+    hbm = pl.BlockSpec(memory_space=pl.ANY)
+    vmem = pl.BlockSpec(memory_space=pltpu.VMEM)
+    smem = pl.BlockSpec(memory_space=pltpu.SMEM)
+    dma = pltpu.SemaphoreType.DMA
+    block = (rows, width)
+    incoming, squares = pl.pallas_call(
+        functools.partial(forward_kernel, fsdp, slots),
+        out_shape=(
+            jax.ShapeDtypeStruct((slots, fsdp) + block, BF),
+            jax.ShapeDtypeStruct((8, 128), F32),
+        ),
+        in_specs=[smem, smem, hbm],
+        out_specs=(hbm, vmem),
+        scratch_shapes=[
+            pltpu.VMEM((block_total,) + block, BF),
+            pltpu.VMEM((steps, 2) + block, BF),
+            pltpu.VMEM((steps, 2) + block, BF),
+            pltpu.VMEM((steps,) + block, BF),
+            pltpu.VMEM((steps,) + block, BF),
+            pltpu.VMEM((steps,) + block, BF),
+            pltpu.VMEM((8, width), F32),
+            pltpu.VMEM((rep, 8, 128), F32),
+            pltpu.VMEM((fsdp, 8, 128), F32),
+            dma,
+            dma((2, steps)),
+            dma((2, steps)),
+            dma((2, steps)),
+            dma((slots,)),
+            dma((2, rep)),
+            dma((2, fsdp)),
+        ],
+        compiler_params=pltpu.CompilerParams(
+            collective_id=0, has_side_effects=True, vmem_limit_bytes=VMEM_BYTES
+        ),
+        name="forward",
+    )(index, valid, partials)
+    clip_limit = 0.5 * math.sqrt(block_total * width * width)
+    returned, fresh = pl.pallas_call(
+        functools.partial(owner_kernel, fsdp, slots, clip_limit),
+        out_shape=(
+            jax.ShapeDtypeStruct((slots, fsdp) + block, BF),
+            jax.ShapeDtypeStruct((slots, width, rank), BF),
+        ),
+        in_specs=[smem, vmem, hbm, vmem],
+        out_specs=(hbm, vmem),
+        scratch_shapes=[
+            pltpu.VMEM((slots, fsdp) + block, BF),
+            pltpu.VMEM((slots, fsdp) + block, BF),
+            pltpu.VMEM((rank, width), BF),
+            pltpu.VMEM((rank, width), BF),
+            pltpu.VMEM((width, rank), F32),
+            pltpu.VMEM((width, rank), F32),
+            pltpu.VMEM((width, rank), BF),
+            dma((slots,)),
+            dma((slots, fsdp)),
+            dma((slots, fsdp)),
+            dma((slots,)),
+        ],
+        compiler_params=pltpu.CompilerParams(
+            collective_id=1, has_side_effects=True, vmem_limit_bytes=VMEM_BYTES
+        ),
+        name="owner",
+    )(active, squares, incoming, sketch[0, 0])
+    returned = returned.reshape((steps,) + block)
+    updates = pl.pallas_call(
+        place_kernel,
+        out_shape=jax.ShapeDtypeStruct((per_slice,) + block, BF),
+        grid_spec=pltpu.PrefetchScalarGridSpec(
+            num_scalar_prefetch=1,
+            grid=(per_slice,),
+            in_specs=[pl.BlockSpec((1,) + block, lambda b, t: (t[b], 0, 0))],
+            out_specs=pl.BlockSpec((1,) + block, lambda b, t: (b, 0, 0)),
+        ),
+        name="place",
+    )(my_target, returned)
+    return (updates, fresh[None, None])
+
+
+VMEM_BYTES = 60 * 1024 * 1024
+
+
+def choose(partials, sketch, owner_table):
+    block_total, rows, width = partials.shape[1:]
+    fsdp = lax.axis_size("fsdp")
+    rep = lax.axis_size("rep")
+    steps = sketch.shape[2] * fsdp
+    pairs = rep == 4 and fsdp & (fsdp - 1) == 0
+    needed = (block_total + 7 * steps) * rows * width * 2
+    if pairs and needed < VMEM_BYTES - (1 << 21):
+        return fused(partials, sketch, owner_table)
+    return local(partials, sketch, owner_table)
+
 
 def solution(mesh):
     placed = (P("rep", None, "fsdp", None), P("fsdp", "rep", None, None, None), P())
     return jax.shard_map(
-        local,
+        choose,
         mesh=mesh,
         in_specs=placed,
         out_specs=(P("rep", "fsdp", None), P("fsdp", "rep", None, None, None)),

time: 448 us -> 247 us (0.55); the launches traced: 441 us -> 247 us
  Pallas kernels: 0 us -> 241 us
  waiting for transfers between devices: 205 us -> 0 us
  blocking collectives: 109 us -> 0 us
  matrix products: 61.9 us -> 0 us
  between operations: 20.1 us -> 0.68 us
  local copies, waits for them, and re-layouts: 21.8 us -> 3.23 us
  other arithmetic: 13.8 us -> 2.2 us
  starting transfers between devices: 10.2 us -> 0 us
    pallas_call x0 -> x3, Pallas kernels: none -> 241 us  [the longest x1 119 us: fused(): pl.pallas_call(functools.partial(forward_kernel, fsdp, slots), out_shape=...]
    reduce_scatter x1 -> x0, waiting for transfers between devices: 118 us -> none  [local(): lax.psum_scatter(partials[0].astype(jnp.float32).astype(jnp.bfloat16), 'r...]
    psum x1 -> x0, blocking collectives: 109 us -> none  [local(): sum_squares = lax.psum(squared_sum(reduced), ('fsdp', 'rep'))]
    all_to_all x2 -> x0, waiting for transfers between devices: 85.5 us -> none  [the longest x1 85.4 us: local(): lax.all_to_all(stacked, 'fsdp', split_axis=1, concat_axis=1, tiled=True)]
    dot_general x82 -> x0, matrix products: 61.9 us -> none  [the longest x20 9.76 us: inverse_root(): jnp.dot(inverse, current, precision=lax.Precision.HIGHEST)]
    unnamed x42 -> x6, local copies, waits for them, and re-layouts: 12.6 us -> 1.49 us
    all_to_all x2 -> x0, starting transfers between devices: 10.2 us -> none  [the longest x1 5.52 us: local(): lax.all_to_all(outgoing, 'fsdp', split_axis=1, concat_axis=1, tiled=True)]
    reshape x2 -> x1, local copies, waits for them, and re-layouts: 6.51 us -> 0.08 us  [fused(): lax.dynamic_index_in_dim(valid, me_r, 0, keepdims=False)]
  transfers between devices with their start and end apart: 3 -> 0, of which waited for: 2 -> 0; matrix products, arithmetic and copies ran while one was open for 3% -> 0% of each run, Pallas kernels for 0% -> 0%
where the time goes in v1:
time: 247 us
  Pallas kernels  241 us (98%)
  local copies, waits for them, and re-layouts  3.23 us (1%)
    pallas_call x1, Pallas kernels, fused(): pl.pallas_call(functools.partial(forward_kernel, fsdp, slots), out_shape=...  119 us
    pallas_call x1, Pallas kernels, fused(): pl.pallas_call(functools.partial(owner_kernel, fsdp, slots, clip_limit),...  112 us
    pallas_call x1, Pallas kernels, fused(): pl.pallas_call(place_kernel, out_shape=jax.ShapeDtypeStruct((per_slice,)...  9.82 us

profile of v1, /device:TPU:0, one launch (start us, length us, event | category | flops | bytes accessed | tf_op | source)
XLA Modules:
  0.0 247.0 jit_solution(17437723994233639438)
XLA Ops:
  0.6 0.5 broadcast.34
  1.1 1.3 reduce.9
  2.5 0.1 eq.28
  2.6 0.1 copy.5
  2.7 0.1 convert_reduce_fusion.1
  2.8 0.6 fusion.target_ref
  3.4 0.1 copy.6
  3.4 0.1 convert_reduce_fusion.valid_ref
  3.5 0.0 copy-start.1
  3.6 0.1 reshape.53
  3.7 0.8 dynamic-slice_reduce_fusion.active_ref
  4.4 0.7 select_reduce_fusion.index_ref
  5.1 0.0 copy-done.1
  5.1 119.1 %forward.1 = (bf16[2,8,128,1024]{3,2,1,0:T(8,128)(2,1)}, f32[8,128]{1,0:T(8,128)}) custom-call(s32[4,16]{1,0:T(4,128)} %select_reduce_fusion.index_ref, f32[4,16]{1,0:T(4,128)} %copy-done.1, bf16[1,56,128,1024]{3,2,1,0:T(8,128)(2,1)} %partials_ref.1), custom_call_target="tpu_custom_call" | custom-call | tf_op jit(solution)/shard_map/forward/pallas_call | solution.py:505
  124.2 112.0 %owner.1 = (bf16[2,8,128,1024]{3,2,1,0:T(8,128)(2,1)}, bf16[2,1024,256]{2,1,0:T(8,128)(2,1)}) custom-call(f32[2]{0:T(128)} %dynamic-slice_reduce_fusion.active_ref, f32[8,128]{1,0:T(8,128)} %get-tuple-element.6.squares_ref, bf16[2,8,128,1024]{3,2,1,0:T(8,128)(2,1)} %get-tuple-element.7.incoming_ref, bf16[2,1024,256]{2,1,0:T(8,128)(2,1)} %bitcast.8), custom_call_target="tpu_custom_call" | custom-call | tf_op jit(solution)/shard_map/owner/pallas_call | solution.py:537
  236.2 0.0 copy-start
  236.2 9.8 %place.1 = bf16[14,128,1024]{2,1,0:T(8,128)(2,1)} custom-call(s32[14]{0:T(128)} %fusion.target_ref, bf16[16,128,1024]{2,1,0:T(8,128)(2,1)} %bitcast.6), custom_call_target="tpu_custom_call" | custom-call | tf_op jit(solution)/shard_map/place/pallas_call | solution.py:564
  246.0 0.0 copy-done
  246.0 1.0 copy.8
  (4 shorter events, 0.0 us)
Async XLA Ops:
  3.5 1.6 copy-start.1
  236.2 9.8 %copy-start = (bf16[2,1024,256]{2,1,0:T(8,128)(2,1)S(1)}, bf16[2,1024,256]{2,1,0:T(8,128)(2,1)}, u32[]{:S(2)}) copy-start(bf16[2,1024,256]{2,1,0:T(8,128)(2,1)} %get-tuple-element.9) | copy-start | bytes 3145732

commit v2 on v0

--- a/solution.py
+++ b/solution.py
@@ -1,8 +1,11 @@
+import functools
 import math
 
 import jax
 import jax.numpy as jnp
 from jax import lax
+from jax.experimental import pallas as pl
+from jax.experimental.pallas import tpu as pltpu
 from jax.sharding import PartitionSpec as P
 
 NS_ITERS = 5
@@ -130,11 +133,487 @@
     my_updates = my_updates.reshape(per_slice, row_count, block_width)
     return (my_updates, jnp.stack(fresh_list)[None, None])
 
+MESH = pl.DeviceIdType.MESH
+BF = jnp.bfloat16
+F32 = jnp.float32
+
+
+def flip(value, mask, bits):
+    result = 0
+    for bit in range(bits):
+        ours = (value // (1 << bit)) % 2
+        theirs = (mask // (1 << bit)) % 2
+        result = result + (ours + theirs - 2 * ours * theirs) * (1 << bit)
+    return result
+
+
+def greet(peers):
+    barrier = pltpu.get_barrier_semaphore()
+    for peer in peers:
+        pl.semaphore_signal(barrier, inc=1, device_id=peer, device_id_type=MESH)
+    pl.semaphore_wait(barrier, len(peers))
+
+
+def remote(source, target, send_sem, recv_sem, peer):
+    return pltpu.make_async_remote_copy(
+        src_ref=source,
+        dst_ref=target,
+        send_sem=send_sem,
+        recv_sem=recv_sem,
+        device_id=peer,
+        device_id_type=MESH,
+    )
+
+
+def mm(a, b):
+    return jnp.dot(a, b, preferred_element_type=F32)
+
+
+def mm_last(a, b):
+    return lax.dot_general(a, b, LAST_AXES, preferred_element_type=F32)
+
+
+def split(values):
+    high = values.astype(BF)
+    return high, (values - high.astype(F32)).astype(BF)
+
+
+def mm3(a, b):
+    return mm(a[0], b[0]) + (mm(a[0], b[1]) + mm(a[1], b[0]))
+
+
+def eye_of(size):
+    return (
+        lax.broadcasted_iota(jnp.int32, (size, size), 0)
+        == lax.broadcasted_iota(jnp.int32, (size, size), 1)
+    ).astype(F32)
+
+
+def kernel_root(matrix, epsilon, identity):
+    trace_sum = jnp.sum(matrix * identity, keepdims=True) + epsilon
+    current = matrix / trace_sum
+    middle = 1.5 * identity - 0.5 * current
+    middle_s = split(middle)
+    inverse_s = middle_s
+    current_s = split(mm3(split(current), middle_s))
+    for repeat in range(1, NS_ITERS):
+        middle_s = split(1.5 * identity - 0.5 * mm3(inverse_s, current_s))
+        if repeat < NS_ITERS - 1:
+            current_s = split(mm3(current_s, middle_s))
+        inverse = mm3(middle_s, inverse_s)
+        inverse_s = split(inverse)
+    return inverse / jnp.sqrt(trace_sum)
+
+
+def step_kernel(
+    fsdp, slots, per_slice, clip_limit, owners_ref, sketch_ref, partials_ref, returned_ref, fresh_ref,
+    held_far, held_own, paired_far, paired_own, far, crossed, summed, incoming, updates, narrow_t, side_t, wide, basis, basis_low,
+    square_acc, rep_squares, fsdp_squares, table, scalars,
+    load_sems, pair_sems, cross_sems, owner_sems, rep_sems, fsdp_sems, home_sems, self_sems, table_sem,
+):
+    bits = fsdp.bit_length() - 1
+    half = fsdp // 2
+    steps = slots * fsdp
+    rows = incoming.shape[2]
+    width = incoming.shape[3]
+    rank = sketch_ref.shape[2]
+    tile = rank
+    me_f = lax.axis_index("fsdp")
+    me_r = lax.axis_index("rep")
+    core = me_r % 2
+    row = me_r // 2
+    partner = row * 2 + 1 - core
+    across = (1 - row) * 2 + core
+    partner_across = (1 - row) * 2 + 1 - core
+
+    def blocks_of(number):
+        return partials_ref.at[0, pl.ds(number * per_slice, per_slice)]
+
+    loads = [
+        pltpu.make_async_copy(blocks_of(across), held_far, load_sems.at[0]),
+        pltpu.make_async_copy(blocks_of(me_r), held_own, load_sems.at[1]),
+    ]
+    pairs = [
+        remote(
+            blocks_of(theirs), landing, pair_sems.at[0, n], pair_sems.at[1, n], {"rep": partner}
+        )
+        for n, (theirs, landing) in enumerate(
+            ((partner_across, paired_far), (partner, paired_own))
+        )
+    ]
+    loads[0].start()
+    fill_table(fsdp, slots, per_slice, owners_ref, table)
+    greet(
+        [{"rep": (me_r + d) % 4} for d in range(1, 4)]
+        + [{"fsdp": (me_f + d) % fsdp} for d in range(1, fsdp)]
+    )
+    pairs[0].start()
+    pairs[1].start()
+    loads[1].start()
+    publish = pltpu.make_async_copy(table, scalars, table_sem)
+    publish.start()
+    square_acc[...] = jnp.zeros_like(square_acc)
+    publish.wait()
+    loads[0].wait()
+    pairs[0].wait_recv()
+
+    def where(i):
+        group = i // (slots * half)
+        slot = (i % (slots * half)) // half
+        mask = fsdp - 1 - half * group - i % half
+        return slot, mask, flip(me_f, mask, bits)
+
+    def cross_copy(i):
+        return remote(
+            far.at[i], crossed.at[i], cross_sems.at[0, i], cross_sems.at[1, i], {"rep": across}
+        )
+
+    def owner_copy(i):
+        slot, mask, owner = where(i)
+        return remote(
+            summed.at[i],
+            incoming.at[slot, me_f],
+            owner_sems.at[0, i],
+            owner_sems.at[1, i],
+            {"fsdp": owner},
+        )
+
+    def send_across(i):
+        slot, mask, owner = where(i)
+        number = scalars[0, across * steps + slot * fsdp + owner]
+        far[i] = (held_far[number].astype(F32) + paired_far[number].astype(F32)).astype(BF)
+        cross_copy(i).start()
+
+    def send_owner(i):
+        slot, mask, owner = where(i)
+        place = me_r * steps + slot * fsdp + owner
+        number = scalars[0, place]
+        cross_copy(i).wait_recv()
+        pair = held_own[number].astype(F32) + paired_own[number].astype(F32)
+        total = (pair + crossed[i].astype(F32)).astype(BF)
+
+        @pl.when(mask == 0)
+        def _():
+            incoming[slot, me_f] = total
+
+        @pl.when(mask != 0)
+        def _():
+            summed[i] = total
+            owner_copy(i).start()
+
+        wide_total = total.astype(F32)
+        folded = jnp.sum((wide_total * wide_total).reshape(rows // 8, 8, width), axis=0)
+        square_acc[...] += jnp.where(scalars[1, place] > 0, folded, 0.0)
+
+    lag = 2
+
+    def first(i, carry):
+        send_across(i)
+        return carry
+
+    lax.fori_loop(0, lag, first, 0)
+    loads[1].wait()
+    pairs[1].wait_recv()
+
+    def both(i, carry):
+        @pl.when(i < steps - lag)
+        def _():
+            send_across(i + lag)
+
+        send_owner(i)
+        return carry
+
+    lax.fori_loop(0, steps, both, 0)
+
+    def arrived(k):
+        def wait_one(n, carry):
+            i = (n // half) * (slots * half) + k * half + n % half
+            owner_copy(i).wait_recv()
+            return carry
+
+        lax.fori_loop(0, fsdp - 1, wait_one, 0)
+
+    def wide_part(k, part):
+        return incoming[k, :, :, part * tile : (part + 1) * tile].reshape(width, tile)
+
+    def project(k, left_t, factor):
+        for part in range(width // tile):
+            product = mm(left_t, wide_part(k, part))
+            if factor is not None:
+                product = factor * product
+            narrow_t[:, part * tile : (part + 1) * tile] = product.astype(BF)
+
+    lanes = square_acc[:, 0:128]
+    for part in range(1, width // 128):
+        lanes = lanes + square_acc[:, part * 128 : (part + 1) * 128]
+    rep_squares[me_r] = lanes
+    rep_copies = [
+        remote(
+            rep_squares.at[me_r], rep_squares.at[me_r], rep_sems.at[0, d], rep_sems.at[1, d],
+            {"rep": (me_r + d) % 4},
+        )
+        for d in range(1, 4)
+    ]
+    for copy in rep_copies:
+        copy.start()
+    arrived(0)
+    sketch_t = sketch_ref[0].T
+    project(0, sketch_t, None)
+    for copy in rep_copies:
+        copy.wait()
+    lanes = rep_squares[0]
+    for r in range(1, 4):
+        lanes = lanes + rep_squares[r]
+    fsdp_squares[me_f] = lanes
+    fsdp_copies = [
+        remote(
+            fsdp_squares.at[me_f], fsdp_squares.at[me_f], fsdp_sems.at[0, d], fsdp_sems.at[1, d],
+            {"fsdp": (me_f + d) % fsdp},
+        )
+        for d in range(1, fsdp)
+    ]
+    for copy in fsdp_copies:
+        copy.start()
+    identity = eye_of(rank)
+
+    def home_copy(k, i):
+        home = flip(me_f, fsdp - 1 - i, bits)
+        return remote(
+            updates.at[k, i], returned_ref.at[k, me_f], home_sems.at[0, k, i], home_sems.at[1, k, i],
+            {"fsdp": home},
+        )
+
+    def self_copy(k):
+        return pltpu.make_async_copy(
+            updates.at[k, fsdp - 1], returned_ref.at[k, me_f], self_sems.at[k]
+        )
+
+    clip_factor = None
+    for k in range(slots):
+        sketch = sketch_ref[k]
+        if k > 0:
+            arrived(k)
+            sketch_t = sketch.T
+            project(k, sketch_t, None)
+        gram = mm(sketch_t, sketch).astype(BF)
+        projected_t = narrow_t[...]
+        for part in range(fsdp):
+            span = slice(part * rows, (part + 1) * rows)
+            wide[span] = mm_last(incoming[k, part], projected_t)
+            basis[span] = DECAY * mm(sketch[span], gram)
+        if k == 0:
+            for copy in fsdp_copies:
+                copy.wait()
+            lanes = fsdp_squares[0]
+            for f in range(1, fsdp):
+                lanes = lanes + fsdp_squares[f]
+            sum_squares = jnp.sum(lanes, keepdims=True)
+            clip_factor = jnp.minimum(1.0, clip_limit / jnp.sqrt(sum_squares + 1e-06))
+        powered_s = split(basis[...] + (clip_factor * clip_factor) * wide[...])
+        powered_t = powered_s[0].T
+        mixed = mm(powered_t, powered_s[1])
+        inner = mm(powered_t, powered_s[0]) + (mixed + mixed.T)
+        root = split(kernel_root(inner, 1e-06, identity))
+        full = mm3(powered_s, root)
+        basis[...] = full
+        low = full.astype(BF)
+        basis_low[...] = low
+        project(k, low.T, clip_factor)
+        coefficients_t = narrow_t[...]
+        align_s = split(mm(sketch_t, low))
+        align_t = (align_s[0].T, align_s[1].T)
+        energy = DECAY * mm3(align_t, align_s) + mm_last(coefficients_t, coefficients_t)
+        root_inverse = kernel_root(energy + DAMPING * identity, 0.0, identity)
+        mix = split(math.sqrt(DAMPING) * root_inverse - identity)
+        side_t[...] = (mm(mix[0], coefficients_t) + mm(mix[1], coefficients_t)).astype(BF)
+
+        def send(i, carry):
+            home = flip(me_f, fsdp - 1 - i, bits)
+            start = pl.multiple_of(home * rows, rows)
+            gradient = (clip_factor * incoming[k, home].astype(F32)).astype(BF).astype(F32)
+            updates[k, i] = (
+                gradient + mm(basis_low[pl.ds(start, rows), :], side_t[...])
+            ).astype(BF)
+
+            @pl.when(i == fsdp - 1)
+            def _():
+                self_copy(k).start()
+
+            @pl.when(i != fsdp - 1)
+            def _():
+                home_copy(k, i).start()
+
+            return carry
+
+        lax.fori_loop(0, fsdp, send, 0)
+        inner_part = split(mm3(split(energy), split(root_inverse)))
+        new_block = mm3(split(basis[...]), inner_part).astype(BF)
+        active = scalars[1, me_r * steps + k * fsdp + me_f]
+        fresh_ref[k] = jnp.where(active > 0, new_block, sketch)
+
+    pairs[0].wait_send()
+    pairs[1].wait_send()
+
+    def finish(i, carry):
+        slot, mask, owner = where(i)
+        cross_copy(i).wait_send()
+
+        @pl.when(mask != 0)
+        def _():
+            owner_copy(i).wait_send()
+
+        return carry
+
+    lax.fori_loop(0, steps, finish, 0)
+
+    def finish_home(i, carry):
+        for k in range(slots):
+            home_copy(k, i).wait()
+        return carry
+
+    lax.fori_loop(0, fsdp - 1, finish_home, 0)
+    for k in range(slots):
+        self_copy(k).wait()
+
+
+def fill_table(fsdp, slots, per_slice, owners_ref, table):
+    total = owners_ref.shape[0]
+    steps = slots * fsdp
+    shape = (total, total)
+    down = lax.broadcasted_iota(jnp.int32, shape, 0)
+    along = lax.broadcasted_iota(jnp.int32, shape, 1)
+    owners = jnp.broadcast_to(owners_ref[...], shape)
+    owners_along = jnp.sum(jnp.where(down == along, owners, 0), axis=0, keepdims=True)
+    slice_down = down // per_slice
+    slice_along = along // per_slice
+    same = (owners == owners_along) & (slice_down == slice_along) & (along < down)
+    ranks = jnp.sum(jnp.where(same, 1, 0), axis=1, keepdims=True)
+    shape = (total, table.shape[1])
+    block = lax.broadcasted_iota(jnp.int32, shape, 0)
+    owned = jnp.broadcast_to(owners_ref[...], shape)
+    target = (block // per_slice) * steps + jnp.broadcast_to(ranks, shape) * fsdp + owned
+    hit = target == lax.broadcasted_iota(jnp.int32, shape, 1)
+    number = jnp.sum(jnp.where(hit, block % per_slice, 0), axis=0, keepdims=True)
+    table[0:1, :] = jnp.minimum(number, per_slice - 1)
+    table[1:2, :] = jnp.sum(jnp.where(hit, 1, 0), axis=0, keepdims=True)
+
+
+def place_kernel(fsdp, per_slice, owners_ref, returned_ref, update_ref, held, counts, in_sems, out_sems):
+    base = lax.axis_index("rep") * per_slice
+    last = returned_ref.shape[0] - 1
+    for owner in range(fsdp):
+        counts[owner] = 0
+    takes, puts = [], []
+    for b in range(per_slice):
+        owner = owners_ref[base + b, 0]
+        count = counts[owner]
+        counts[owner] = count + 1
+        takes.append(
+            pltpu.make_async_copy(returned_ref.at[jnp.minimum(count, last), owner], held.at[b], in_sems.at[b])
+        )
+        takes[-1].start()
+    for b in range(per_slice):
+        takes[b].wait()
+        puts.append(pltpu.make_async_copy(held.at[b], update_ref.at[b], out_sems.at[b]))
+        puts[-1].start()
+    for put in puts:
+        put.wait()
+
+
+def fused(partials, sketch, owner_table):
+    block_total, rows, width = partials.shape[1:]
+    rank = sketch.shape[4]
+    fsdp = lax.axis_size("fsdp")
+    rep = lax.axis_size("rep")
+    slots = sketch.shape[2]
+    per_slice = block_total // rep
+    steps = slots * fsdp
+    table_width = -(-rep * steps // 128) * 128
+    hbm = pl.BlockSpec(memory_space=pl.ANY)
+    vmem = pl.BlockSpec(memory_space=pltpu.VMEM)
+    smem = pl.BlockSpec(memory_space=pltpu.SMEM)
+    dma = pltpu.SemaphoreType.DMA
+    block = (rows, width)
+    clip_limit = 0.5 * math.sqrt(block_total * width * width)
+    returned, fresh = pl.pallas_call(
+        functools.partial(step_kernel, fsdp, slots, per_slice, clip_limit),
+        out_shape=(
+            jax.ShapeDtypeStruct((slots, fsdp) + block, BF),
+            jax.ShapeDtypeStruct((slots, width, rank), BF),
+        ),
+        in_specs=[vmem, vmem, hbm],
+        out_specs=(hbm, vmem),
+        scratch_shapes=[
+            pltpu.VMEM((per_slice,) + block, BF),
+            pltpu.VMEM((per_slice,) + block, BF),
+            pltpu.VMEM((per_slice,) + block, BF),
+            pltpu.VMEM((per_slice,) + block, BF),
+            pltpu.VMEM((steps,) + block, BF),
+            pltpu.VMEM((steps,) + block, BF),
+            pltpu.VMEM((steps,) + block, BF),
+            pltpu.VMEM((slots, fsdp) + block, BF),
+            pltpu.VMEM((slots, fsdp) + block, BF),
+            pltpu.VMEM((rank, width), BF),
+            pltpu.VMEM((rank, width), BF),
+            pltpu.VMEM((width, rank), F32),
+            pltpu.VMEM((width, rank), F32),
+            pltpu.VMEM((width, rank), BF),
+            pltpu.VMEM((8, width), F32),
+            pltpu.VMEM((rep, 8, 128), F32),
+            pltpu.VMEM((fsdp, 8, 128), F32),
+            pltpu.VMEM((2, table_width), jnp.int32),
+            pltpu.SMEM((2, table_width), jnp.int32),
+            dma((2,)),
+            dma((2, 2)),
+            dma((2, steps)),
+            dma((2, steps)),
+            dma((2, rep)),
+            dma((2, fsdp)),
+            dma((2, slots, fsdp)),
+            dma((slots,)),
+            dma,
+        ],
+        compiler_params=pltpu.CompilerParams(
+            collective_id=0, has_side_effects=True, vmem_limit_bytes=VMEM_BYTES
+        ),
+        name="step",
+    )(owner_table, sketch[0, 0], partials)
+    updates = pl.pallas_call(
+        functools.partial(place_kernel, fsdp, per_slice),
+        out_shape=jax.ShapeDtypeStruct((per_slice,) + block, BF),
+        in_specs=[smem, hbm],
+        out_specs=hbm,
+        scratch_shapes=[
+            pltpu.VMEM((per_slice,) + block, BF),
+            pltpu.SMEM((fsdp,), jnp.int32),
+            dma((per_slice,)),
+            dma((per_slice,)),
+        ],
+        name="place",
+    )(owner_table, returned)
+    return (updates, fresh[None, None])
+
+
+VMEM_BYTES = 60 * 1024 * 1024
+
+
+def choose(partials, sketch, owner_table):
+    block_total, rows, width = partials.shape[1:]
+    fsdp = lax.axis_size("fsdp")
+    rep = lax.axis_size("rep")
+    steps = sketch.shape[2] * fsdp
+    per_slice = block_total // rep
+    pairs = rep == 4 and fsdp & (fsdp - 1) == 0
+    needed = (4 * per_slice + 5 * steps) * rows * width * 2
+    if pairs and needed < VMEM_BYTES - (12 << 20):
+        return fused(partials, sketch, owner_table)
+    return local(partials, sketch, owner_table)
+
 
 def solution(mesh):
     placed = (P("rep", None, "fsdp", None), P("fsdp", "rep", None, None, None), P())
     return jax.shard_map(
-        local,
+        choose,
         mesh=mesh,
         in_specs=placed,
         out_specs=(P("rep", "fsdp", None), P("fsdp", "rep", None, None, None)),

time: 448 us -> 233 us (0.52); the launches traced: 441 us -> 233 us
  Pallas kernels: 0 us -> 230 us
  waiting for transfers between devices: 205 us -> 0 us
  blocking collectives: 109 us -> 0 us
  matrix products: 61.9 us -> 0 us
  local copies, waits for them, and re-layouts: 21.8 us -> 2.33 us
  between operations: 20.1 us -> 0.66 us
  other arithmetic: 13.8 us -> 0 us
  starting transfers between devices: 10.2 us -> 0 us
    pallas_call x0 -> x2, Pallas kernels: none -> 230 us  [the longest x1 225 us: fused(): pl.pallas_call(functools.partial(step_kernel, fsdp, slots, per_slice, cli...]
    reduce_scatter x1 -> x0, waiting for transfers between devices: 118 us -> none  [local(): lax.psum_scatter(partials[0].astype(jnp.float32).astype(jnp.bfloat16), 'r...]
    psum x1 -> x0, blocking collectives: 109 us -> none  [local(): sum_squares = lax.psum(squared_sum(reduced), ('fsdp', 'rep'))]
    all_to_all x2 -> x0, waiting for transfers between devices: 85.5 us -> none  [the longest x1 85.4 us: local(): lax.all_to_all(stacked, 'fsdp', split_axis=1, concat_axis=1, tiled=True)]
    dot_general x82 -> x0, matrix products: 61.9 us -> none  [the longest x20 9.76 us: inverse_root(): jnp.dot(inverse, current, precision=lax.Precision.HIGHEST)]
    unnamed x42 -> x4, local copies, waits for them, and re-layouts: 12.6 us -> 2.33 us
    all_to_all x2 -> x0, starting transfers between devices: 10.2 us -> none  [the longest x1 5.52 us: local(): lax.all_to_all(outgoing, 'fsdp', split_axis=1, concat_axis=1, tiled=True)]
    reshape x2 -> x0, local copies, waits for them, and re-layouts: 6.51 us -> none  [the longest x1 4.3 us: local(): outgoing = outgoing.reshape(slot_count, fsdp_count, row_count, block_width)]
  transfers between devices with their start and end apart: 3 -> 0, of which waited for: 2 -> 0; matrix products, arithmetic and copies ran while one was open for 3% -> 0% of each run, Pallas kernels for 0% -> 0%
where the time goes in v2:
time: 233 us
  Pallas kernels  230 us (99%)
  local copies, waits for them, and re-layouts  2.33 us (1%)
    pallas_call x1, Pallas kernels, fused(): pl.pallas_call(functools.partial(step_kernel, fsdp, slots, per_slice, cli...  225 us

profile of v2, /device:TPU:0, one launch (start us, length us, event | category | flops | bytes accessed | tf_op | source)
XLA Modules:
  0.0 233.0 jit_solution(8005124944476447050)
XLA Ops:
  0.6 1.4 copy.6.owners_ref
  2.0 225.4 %step.1 = (bf16[2,8,128,1024]{3,2,1,0:T(8,128)(2,1)}, bf16[2,1024,256]{2,1,0:T(8,128)(2,1)}) custom-call(s32[56,1]{1,0:T(8,128)} %copy.6.owners_ref, bf16[2,1024,256]{2,1,0:T(8,128)(2,1)} %bitcast.2, bf16[1,56,128,1024]{3,2,1,0:T(8,128)(2,1)} %partials_ref.1), custom_call_target="tpu_custom_call" | custom-call | tf_op jit(solution)/shard_map/step/pallas_call | solution.py:538
  227.4 0.0 copy-start
  227.4 4.5 %place.1 = bf16[14,128,1024]{2,1,0:T(8,128)(2,1)} custom-call(s32[56,1]{1,0:T(8,128)} %copy.6.owners_ref, bf16[2,8,128,1024]{3,2,1,0:T(8,128)(2,1)} %get-tuple-element.4.returned_ref), custom_call_target="tpu_custom_call" | custom-call | tf_op jit(solution)/shard_map/place/pallas_call | solution.py:581
  232.0 0.0 copy-done
  232.0 1.0 copy.8
Async XLA Ops:
  227.4 4.6 %copy-start = (bf16[2,1024,256]{2,1,0:T(8,128)(2,1)S(1)}, bf16[2,1024,256]{2,1,0:T(8,128)(2,1)}, u32[]{:S(2)}) copy-start(bf16[2,1024,256]{2,1,0:T(8,128)(2,1)} %get-tuple-element.5) | copy-start | bytes 3145732
